TPU v7x, 32 devices: a whole 2x2x4 slice. The times are simulated.
32 devices in a mesh: rep: 2 (over x), shard: 16 (over z, y, core).
Axes of the slice: x: 2, y: 2, z: 4, core: 2. Of those that a mesh axis runs over, the one named last changes fastest.
Arguments:
- tokens_x: bfloat16 [8192, 4096], P(('rep', 'shard')), may hold values from -6 to 6
- key_grad: bfloat16 [8192, 1024], P(('rep', 'shard')), may hold values from -0.06591797 to 0.06591797
- left_root: bfloat16 [64, 512, 512], P('shard'), may hold values from -1 to 3
- slot_grads: bfloat16 [64, 512, 512], P('shard'), may hold values from -6 to 6
- right_root: bfloat16 [64, 512, 512], P('shard'), may hold values from -1 to 3
- block_slot: int32 [32], replicated, may hold values from 0 to 63, as said below
Outputs:
- grad_key: float32 [4096, 1024], P('shard')
- update: bfloat16 [512, 32, 512], P('shard')
Inputs may be any that keep to these rules, and one draw needn't show every extreme that they name: `block_slot`: the entries are distinct; slot v is slot v % 4 of shard index v // 4; no shard index holds more than 4 blocks, and some shard index holds exactly 4.
All inputs are finite; a program needn't handle non-finite values.
Results may differ from a plain program's by a relative error of at most 0.006.
Values may be sent and summed in bfloat16 or wider, within the bound.
A program may use at most 128 MiB of HBM per device.

v0:
```python
import jax
import jax.numpy as jnp
from jax import lax
from jax.sharding import PartitionSpec as P


def column_term(features, cotangent):
    return lax.dot_general(
        features, cotangent, (((0,), (0,)), ((), ())), preferred_element_type=jnp.float32
    )


def precondition(left_block, grad_block, right_block):
    left_part = jnp.einsum(
        "sij,sjk->sik", left_block, grad_block, preferred_element_type=jnp.float32
    ).astype(jnp.bfloat16)
    return jnp.einsum(
        "sij,sjk->isk", left_part, right_block, preferred_element_type=jnp.float32
    ).astype(jnp.bfloat16)


def shards(tokens_x, key_grad, left_root, slot_grads, right_root, block_slot):
    n_shard = lax.axis_size("shard")
    n_rep = lax.axis_size("rep")
    own_rows = lax.psum_scatter(
        column_term(tokens_x, key_grad), "shard", scatter_dimension=0, tiled=True
    )
    grad_key = lax.psum(own_rows, "rep")
    slot_count = left_root.shape[0]
    half_slots = slot_count // n_rep
    first_slot = lax.axis_index("rep") * half_slots

    def own_half(values):
        return lax.dynamic_slice_in_dim(values, first_slot, half_slots, 0)

    product = precondition(own_half(left_root), own_half(slot_grads), own_half(right_root))
    received = lax.all_to_all(product, "shard", split_axis=0, concat_axis=1, tiled=True)
    joined = lax.all_gather(received, "rep", axis=1, tiled=True)
    owner = block_slot // slot_count
    within = block_slot % slot_count
    position = (
        within // half_slots * (n_shard * half_slots) + owner * half_slots + within % half_slots
    )
    update = jnp.take(joined, position, axis=1)
    return (grad_key, update)


def solution(mesh):
    return jax.shard_map(
        shards,
        mesh=mesh,
        in_specs=(
            P(("rep", "shard"), None),
            P(("rep", "shard"), None),
            P("shard", None, None),
            P("shard", None, None),
            P("shard", None, None),
            P(),
        ),
        out_specs=(P("shard", None), P("shard", None, None)),
        check_vma=False,
    )
```

profile of v0, /device:TPU:0, one launch (start us, length us, event | category | flops | bytes accessed | tf_op | source)
XLA Modules:
  0.0 247.9 jit_solution(18152596970215478150)
XLA Ops:
  8.0 0.0 copy-start
  8.0 0.0 reduce-scatter.2.cloned.1.call-start
  8.1 1.5 copy-done
  9.6 9.2 %fusion.9 = f32[4096,1024]{1,0:T(8,128)} fusion(bf16[256,4096]{1,0:T(8,128)(2,1)S(1)} %copy-done, bf16[256,1024]{1,0:T(8,128)(2,1)} %param.7), kind=kOutput, calls=%fused_computation.23 | convolution fusion | flops 2147483648 | bytes 19398656 | tf_op jit(solution)/shard_map/dot_general | solution.py:8
  18.8 0.0 reduce-scatter.2.cloned.1.call-update
  18.8 0.0 all-gather.2.cloned.1.call-start
  18.8 4.1 %fusion = bf16[512,2,512]{0,2,1:T(8,128)(2,1)} fusion(bf16[4,512,512]{2,1,0:T(8,128)(2,1)} %param.9, s32[]{:T(128)S(6)} %select_n.37, bf16[4,512,512]{2,1,0:T(8,128)(2,1)} %param.8, bf16[4,512,512]{2,1,0:T(8,128)(2,1)} %param.10), kind=kOutput, calls=%fused_computation.3 | convolution fusion | flops 1074790400 | bytes 4195840 | tf_op jit(solution)/shard_map/sij,sjk->isk/dot_general | solution.py:17
  22.9 2.5 %copy.14 = bf16[512,2,512]{2,1,0:T(2,128)(2,1)S(1)} copy(bf16[512,2,512]{0,2,1:T(8,128)(2,1)} %fusion) | data formatting | bytes 2097152 | tf_op jit(solution)/shard_map/convert_element_type | solution.py:19
  25.4 31.9 %all_to_all.18 = bf16[512,2,512]{2,1,0:T(2,128)(2,1)S(1)} all-to-all(bf16[512,2,512]{2,1,0:T(2,128)(2,1)S(1)} %copy.14), channel_id=1, replica_groups=mesh['rep'=2,'shard'=16] {'shard'}, dimensions={0} | all-to-all | bytes 2097152 | tf_op jit(solution)/shard_map/all_to_all | solution.py:37
  57.3 0.2 copy.15
  57.5 0.0 copy-start.1
  57.5 1.0 copy.16
  58.6 0.0 all-gather.2.cloned.1.call-update
  58.6 0.0 all-reduce.2.cloned.1.call-start
  58.6 140.4 %reduce-scatter.2.cloned.1.call-done = f32[256,1024]{1,0:T(8,128)} async-done(((f32[4096,1024]{1,0:T(8,128)}), f32[256,1024]{1,0:T(8,128)}) %reduce-scatter.2.cloned.1.call-update) | async-done | bytes 1048592 | tf_op jit(solution)/shard_map/reduce_scatter | solution.py:25
  199.0 0.0 all-reduce.2.cloned.1.call-update
  199.0 0.0 copy-done.1
  199.1 0.0 all-gather.2.cloned.1.call-done
  199.1 2.2 gather_fusion
  201.3 0.2 select_bitcast_fusion
  201.5 1.5 copy.17
  203.0 35.1 %all-reduce.2.cloned.1.call-done = f32[256,1024]{1,0:T(8,128)} async-done(((f32[256,1024]{1,0:T(8,128)}), f32[256,1024]{1,0:T(8,128)}) %all-reduce.2.cloned.1.call-update) | async-done | bytes 1048592 | tf_op jit(solution)/shard_map/psum | solution.py:28
  238.2 2.3 copy.20
  (2 shorter events, 0.0 us)
Async XLA Ops:
  8.0 1.6 copy-start
  8.0 191.0 %reduce-scatter.2.cloned.1.call-start = ((), (), s32[]{:S(2)}) async-start(), calls=%async_computation.2 | async-start | bytes 17825792 | tf_op jit(solution)/shard_map/reduce_scatter | solution.py:25
  18.8 180.3 %all-gather.2.cloned.1.call-start = ((), (), s32[]{:S(2)}) async-start(), calls=%async_computation.4 | async-start | bytes 3145728 | tf_op jit(solution)/shard_map/all_gather | solution.py:38
  57.5 141.5 %copy-start.1 = (s32[32]{0:T(128)S(1)}, s32[32]{0:T(128)}, u32[]{:S(2)}) copy-start(s32[32]{0:T(128)} %param.11) | copy-start | bytes 388
  58.6 179.6 %all-reduce.2.cloned.1.call-start = ((), (), s32[]{:S(2)}) async-start(), calls=%async_computation.3 | async-start | bytes 2097152 | tf_op jit(solution)/shard_map/psum | solution.py:28
Sparse Core Ops, SparseCore 0:
  18.9 180.0 reduce-scatter.1
Sparse Core Ops, SparseCore 1:
  58.7 33.3 all-gather.1
  199.1 39.0 all-reduce.1
where the time goes:
time: 248 us
  waiting for transfers between devices  176 us (71%)
  blocking collectives  31.9 us (13%)
  between operations  15.6 us (6%)
  matrix products  13.3 us (5%)
  local copies, waits for them, and re-layouts  11.3 us (5%)
    reduce_scatter x1, waiting for transfers between devices, shards(): lax.psum_scatter(column_term(tokens_x, key_grad), 'shard', scatter_dimens...  140 us
    psum x1, waiting for transfers between devices, shards(): grad_key = lax.psum(own_rows, 'rep')  35.1 us
    all_to_all x1, blocking collectives, shards(): lax.all_to_all(product, 'shard', split_axis=0, concat_axis=1, tiled=True)  31.9 us
    dot_general x1, matrix products, column_term(): lax.dot_general(features, cotangent, (((0,), (0,)), ((), ())), preferred_...  9.16 us
    unnamed x6, local copies, waits for them, and re-layouts  5.4 us
  transfers between devices with their start and end apart: 3, of which 2 were waited for; matrix products, arithmetic and copies ran while one was open for 5% of the time, Pallas kernels for 0%

commit v1 on v0

--- a/solution.py
+++ b/solution.py
@@ -2,6 +2,23 @@
 import jax.numpy as jnp
 from jax import lax
 from jax.sharding import PartitionSpec as P
+
+
+def loops_wrap(local, which_dim, s0):
+    tall = local.shape
+    lower = jnp.moveaxis(
+        local.reshape(*tall[:which_dim], s0, tall[which_dim] // s0, *tall[which_dim + 1 :]),
+        which_dim,
+        0,
+    )
+    return lower
+
+
+def mix_the_seats_all(load, in_dim):
+    s_next = list(load.shape[1:])
+    s_next[in_dim] *= load.shape[0]
+    local_out = jnp.moveaxis(load, 0, in_dim).reshape(s_next)
+    return local_out
 
 
 def column_term(features, cotangent):
@@ -34,7 +51,20 @@
         return lax.dynamic_slice_in_dim(values, first_slot, half_slots, 0)
 
     product = precondition(own_half(left_root), own_half(slot_grads), own_half(right_root))
-    received = lax.all_to_all(product, "shard", split_axis=0, concat_axis=1, tiled=True)
+    block_out, left_arr = (lax.axis_size("shard"), lax.axis_index("shard"))
+    last = loops_wrap(product, 0, block_out)
+    heap = [last[left_arr]]
+    for num in range(1, block_out):
+        shaped = last[(left_arr + num) % block_out]
+        heap.append(
+            lax.ppermute(
+                shaped,
+                axis_name="shard",
+                perm=[(i, (i + num) % block_out) for i in range(block_out)],
+            )
+        )
+    last = jnp.stack(heap, axis=0)[(left_arr - jnp.arange(block_out)) % block_out]
+    received = mix_the_seats_all(last, 1)
     joined = lax.all_gather(received, "rep", axis=1, tiled=True)
     owner = block_slot // slot_count
     within = block_slot % slot_count

time: 248 us -> 248 us (level)
  blocking collectives: 31.9 us -> 0 us
  starting transfers between devices: 0.13 us -> 21.9 us
  waiting for transfers between devices: 176 us -> 186 us
    all_to_all x1 -> x0, blocking collectives: 31.9 us -> none  [shards(): lax.all_to_all(product, 'shard', split_axis=0, concat_axis=1, tiled=True)]
    ppermute x0 -> x15, starting transfers between devices: none -> 21.7 us  [shards(): lax.ppermute(shaped, axis_name='shard', perm=[(i, (i + num) % block_out)...]
    ppermute x0 -> x15, waiting for transfers between devices: none -> 9.69 us  [shards(): lax.ppermute(shaped, axis_name='shard', perm=[(i, (i + num) % block_out)...]
    convert_element_type x1 -> x0, local copies, waits for them, and re-layouts: 2.5 us -> none  [precondition(): return jnp.einsum('sij,sjk->isk', left_part, right_block, preferred_eleme...]
    unnamed x6 -> x20, local copies, waits for them, and re-layouts: 5.4 us -> 5.48 us
  transfers between devices with their start and end apart: 3 -> 18, of which waited for: 2 -> 7; matrix products, arithmetic and copies ran while one was open for 5% -> 4% of each run, Pallas kernels for 0% -> 0%
where the time goes in v1:
time: 248 us
  waiting for transfers between devices  186 us (75%)
  starting transfers between devices  21.9 us (9%)
  between operations  15.9 us (6%)
  matrix products  13.2 us (5%)
  local copies, waits for them, and re-layouts  10.6 us (4%)
    reduce_scatter x1, waiting for transfers between devices, shards(): lax.psum_scatter(column_term(tokens_x, key_grad), 'shard', scatter_dimens...  141 us
    psum x1, waiting for transfers between devices, shards(): grad_key = lax.psum(own_rows, 'rep')  35.1 us
    ppermute x15, starting transfers between devices, shards(): lax.ppermute(shaped, axis_name='shard', perm=[(i, (i + num) % block_out)...  21.7 us
    ppermute x15, waiting for transfers between devices, shards(): lax.ppermute(shaped, axis_name='shard', perm=[(i, (i + num) % block_out)...  9.69 us
    dot_general x1, matrix products, column_term(): lax.dot_general(features, cotangent, (((0,), (0,)), ((), ())), preferred_...  9.16 us
    unnamed x20, local copies, waits for them, and re-layouts  5.48 us
  transfers between devices with their start and end apart: 18, of which 7 were waited for; matrix products, arithmetic and copies ran while one was open for 4% of the time, Pallas kernels for 0%

profile of v1, /device:TPU:0, one launch (start us, length us, event | category | flops | bytes accessed | tf_op | source)
XLA Modules:
  0.0 247.9 jit_solution(5651827824811297885)
XLA Ops:
  8.0 0.0 copy-start
  8.0 0.0 reduce-scatter.2.cloned.1.call-start
  8.1 1.5 copy-done
  9.6 9.2 %fusion.10 = f32[4096,1024]{1,0:T(8,128)} fusion(bf16[256,4096]{1,0:T(8,128)(2,1)S(1)} %copy-done, bf16[256,1024]{1,0:T(8,128)(2,1)} %param.7), kind=kOutput, calls=%fused_computation.61 | convolution fusion | flops 2147483648 | bytes 19398656 | tf_op jit(solution)/shard_map/dot_general | solution.py:25
  18.7 0.0 reduce-scatter.2.cloned.1.call-update
  18.8 0.0 all-gather.2.cloned.1.call-start
  19.1 4.1 %convolution_convert_fusion = bf16[2,512,512]{1,2,0:T(8,128)(2,1)} fusion(bf16[4,512,512]{2,1,0:T(8,128)(2,1)} %param.9, s32[]{:T(128)S(6)} %select_n.170, bf16[4,512,512]{2,1,0:T(8,128)(2,1)} %param.8, bf16[4,512,512]{2,1,0:T(8,128)(2,1)} %param.10), kind=kOutput, calls=%fused_computation.2 | convolution fusion | flops 1074790400 | bytes 4195840 | tf_op jit(solution)/shard_map/sij,sjk->isk/dot_general | solution.py:34
  23.2 1.4 dynamic-slice_bitcast_fusion
  24.5 0.5 collective-permute-start
  25.1 2.6 %collective-permute-start.1 = (bf16[32,2,512]{2,0,1:T(8,128)(2,1)S(1)}, bf16[32,2,512]{2,0,1:T(8,128)(2,1)S(1)}, u32[]{:S(2)}, u32[]{:S(2)}) collective-permute-start(bf16[32,2,512]{2,0,1:T(8,128)(2,1)S(1)} %get-tuple-element.21), channel_id=1, source_target_pairs={{0,2},{1,3},{2,4},{3,5},{4,6},{5,7},{6,8},{7,9},{8,10},{9,11},{10,... | collective-permute-start | bytes 196616 | tf_op jit(solution)/shard_map/ppermute | solution.py:60
  27.6 2.4 collective-permute-start.2
  30.1 1.6 collective-permute-start.3
  31.6 0.2 collective-permute-start.4
  31.8 0.2 collective-permute-done
  32.0 1.1 collective-permute-start.5
  33.1 0.0 collective-permute-done.1
  33.1 4.4 %collective-permute-start.6 = (bf16[32,2,512]{2,0,1:T(8,128)(2,1)S(1)}, bf16[32,2,512]{2,0,1:T(8,128)(2,1)S(1)}, u32[]{:S(2)}, u32[]{:S(2)}) collective-permute-start(bf16[32,2,512]{2,0,1:T(8,128)(2,1)S(1)} %get-tuple-element.16), channel_id=1, source_target_pairs={{0,7},{1,8},{2,9},{3,10},{4,11},{5,12},{6,13},{7,14},{8,15},{9,0},... | collective-permute-start | bytes 196616 | tf_op jit(solution)/shard_map/ppermute | solution.py:60
  37.5 0.0 collective-permute-done.2
  37.5 0.4 collective-permute-start.7
  37.9 0.0 collective-permute-done.3
  37.9 0.3 collective-permute-start.8
  38.3 6.6 %collective-permute-done.4 = bf16[32,2,512]{2,0,1:T(8,128)(2,1)S(1)} collective-permute-done((bf16[32,2,512]{2,0,1:T(8,128)(2,1)S(1)}, bf16[32,2,512]{2,0,1:T(8,128)(2,1)S(1)}, u32[]{:S(2)}, u32[]{:S(2)}) %collective-permute-start.4) | collective-permute-done | bytes 65568 | tf_op jit(solution)/shard_map/ppermute | solution.py:60
  44.8 0.0 collective-permute-start.9
  44.8 0.2 collective-permute-done.5
  45.0 0.4 collective-permute-start.10
  45.4 0.0 collective-permute-done.6
  45.4 1.9 collective-permute-start.11
  47.3 0.0 collective-permute-done.7
  47.3 2.2 collective-permute-start.12
  49.5 0.0 collective-permute-done.8
  49.5 3.4 %collective-permute-start.13 = (bf16[32,2,512]{2,0,1:T(8,128)(2,1)S(1)}, bf16[32,2,512]{2,0,1:T(8,128)(2,1)S(1)}, u32[]{:S(2)}, u32[]{:S(2)}) collective-permute-start(bf16[32,2,512]{2,0,1:T(8,128)(2,1)S(1)} %get-tuple-element.9), channel_id=1, source_target_pairs={{0,14},{1,15},{2,0},{3,1},{4,2},{5,3},{6,4},{7,5},{8,6},{9,7},{10,... | collective-permute-start | bytes 196616 | tf_op jit(solution)/shard_map/ppermute | solution.py:60
  52.9 0.0 collective-permute-done.9
  52.9 0.4 collective-permute-start.14
  53.3 0.0 collective-permute-done.10
  53.4 0.0 collective-permute-done.12
  53.4 2.3 collective-permute-done.13
  55.7 0.4 collective-permute-done.14
  56.2 1.6 gather_fusion
  57.7 0.0 all-gather.2.cloned.1.call-update
  57.8 0.0 all-reduce.2.cloned.1.call-start
  57.8 141.2 %reduce-scatter.2.cloned.1.call-done = f32[256,1024]{1,0:T(8,128)} async-done(((f32[4096,1024]{1,0:T(8,128)}), f32[256,1024]{1,0:T(8,128)}) %reduce-scatter.2.cloned.1.call-update) | async-done | bytes 1048592 | tf_op jit(solution)/shard_map/reduce_scatter | solution.py:42
  199.0 0.0 all-reduce.2.cloned.1.call-update
  199.1 0.0 all-gather.2.cloned.1.call-done
  199.1 2.2 gather_fusion.1
  201.3 0.2 select_bitcast_fusion
  201.5 1.5 copy.9
  203.0 35.1 %all-reduce.2.cloned.1.call-done = f32[256,1024]{1,0:T(8,128)} async-done(((f32[256,1024]{1,0:T(8,128)}), f32[256,1024]{1,0:T(8,128)}) %all-reduce.2.cloned.1.call-update) | async-done | bytes 1048592 | tf_op jit(solution)/shard_map/psum | solution.py:45
  238.1 2.3 copy.26
  (22 shorter events, 0.1 us)
Async XLA Ops:
  8.0 1.6 copy-start
  8.0 191.0 %reduce-scatter.2.cloned.1.call-start = ((), (), s32[]{:S(2)}) async-start(), calls=%async_computation.1 | async-start | bytes 17825792 | tf_op jit(solution)/shard_map/reduce_scatter | solution.py:42
  18.8 180.3 %all-gather.2.cloned.1.call-start = ((), (), s32[]{:S(2)}) async-start(), calls=%async_computation.3 | async-start | bytes 3145728 | tf_op jit(solution)/shard_map/all_gather | solution.py:68
  24.5 7.5 %collective-permute-start = (bf16[32,2,512]{2,0,1:T(8,128)(2,1)S(1)}, bf16[32,2,512]{2,0,1:T(8,128)(2,1)S(1)}, u32[]{:S(2)}, u32[]{:S(2)}) collective-permute-start(bf16[32,2,512]{2,0,1:T(8,128)(2,1)S(1)} %get-tuple-element.22), channel_id=1, source_target_pairs={{0,1},{1,2},{2,3},{3,4},{4,5},{5,6},{6,7},{7,8},{8,9},{9,10},{10,1... | collective-permute-start | bytes 196616 | tf_op jit(solution)/shard_map/ppermute | solution.py:60
  25.1 8.0 %collective-permute-start.1 = (bf16[32,2,512]{2,0,1:T(8,128)(2,1)S(1)}, bf16[32,2,512]{2,0,1:T(8,128)(2,1)S(1)}, u32[]{:S(2)}, u32[]{:S(2)}) collective-permute-start(bf16[32,2,512]{2,0,1:T(8,128)(2,1)S(1)} %get-tuple-element.21), channel_id=1, source_target_pairs={{0,2},{1,3},{2,4},{3,5},{4,6},{5,7},{6,8},{7,9},{8,10},{9,11},{10,... | collective-permute-start | bytes 196616 | tf_op jit(solution)/shard_map/ppermute | solution.py:60
  27.6 9.8 %collective-permute-start.2 = (bf16[32,2,512]{2,0,1:T(8,128)(2,1)S(1)}, bf16[32,2,512]{2,0,1:T(8,128)(2,1)S(1)}, u32[]{:S(2)}, u32[]{:S(2)}) collective-permute-start(bf16[32,2,512]{2,0,1:T(8,128)(2,1)S(1)} %get-tuple-element.20), channel_id=1, source_target_pairs={{0,3},{1,4},{2,5},{3,6},{4,7},{5,8},{6,9},{7,10},{8,11},{9,12},{10... | collective-permute-start | bytes 196616 | tf_op jit(solution)/shard_map/ppermute | solution.py:60
  30.1 7.8 %collective-permute-start.3 = (bf16[32,2,512]{2,0,1:T(8,128)(2,1)S(1)}, bf16[32,2,512]{2,0,1:T(8,128)(2,1)S(1)}, u32[]{:S(2)}, u32[]{:S(2)}) collective-permute-start(bf16[32,2,512]{2,0,1:T(8,128)(2,1)S(1)} %get-tuple-element.19), channel_id=1, source_target_pairs={{0,4},{1,5},{2,6},{3,7},{4,8},{5,9},{6,10},{7,11},{8,12},{9,13},{1... | collective-permute-start | bytes 196616 | tf_op jit(solution)/shard_map/ppermute | solution.py:60
  31.6 13.2 %collective-permute-start.4 = (bf16[32,2,512]{2,0,1:T(8,128)(2,1)S(1)}, bf16[32,2,512]{2,0,1:T(8,128)(2,1)S(1)}, u32[]{:S(2)}, u32[]{:S(2)}) collective-permute-start(bf16[32,2,512]{2,0,1:T(8,128)(2,1)S(1)} %get-tuple-element.18), channel_id=1, source_target_pairs={{0,5},{1,6},{2,7},{3,8},{4,9},{5,10},{6,11},{7,12},{8,13},{9,14},{... | collective-permute-start | bytes 196616 | tf_op jit(solution)/shard_map/ppermute | solution.py:60
  32.0 13.0 %collective-permute-start.5 = (bf16[32,2,512]{2,0,1:T(8,128)(2,1)S(1)}, bf16[32,2,512]{2,0,1:T(8,128)(2,1)S(1)}, u32[]{:S(2)}, u32[]{:S(2)}) collective-permute-start(bf16[32,2,512]{2,0,1:T(8,128)(2,1)S(1)} %get-tuple-element.17), channel_id=1, source_target_pairs={{0,6},{1,7},{2,8},{3,9},{4,10},{5,11},{6,12},{7,13},{8,14},{9,15},... | collective-permute-start | bytes 196616 | tf_op jit(solution)/shard_map/ppermute | solution.py:60
  33.1 12.3 %collective-permute-start.6 = (bf16[32,2,512]{2,0,1:T(8,128)(2,1)S(1)}, bf16[32,2,512]{2,0,1:T(8,128)(2,1)S(1)}, u32[]{:S(2)}, u32[]{:S(2)}) collective-permute-start(bf16[32,2,512]{2,0,1:T(8,128)(2,1)S(1)} %get-tuple-element.16), channel_id=1, source_target_pairs={{0,7},{1,8},{2,9},{3,10},{4,11},{5,12},{6,13},{7,14},{8,15},{9,0},... | collective-permute-start | bytes 196616 | tf_op jit(solution)/shard_map/ppermute | solution.py:60
  37.5 9.8 %collective-permute-start.7 = (bf16[32,2,512]{2,0,1:T(8,128)(2,1)S(1)}, bf16[32,2,512]{2,0,1:T(8,128)(2,1)S(1)}, u32[]{:S(2)}, u32[]{:S(2)}) collective-permute-start(bf16[32,2,512]{2,0,1:T(8,128)(2,1)S(1)} %get-tuple-element.15), channel_id=1, source_target_pairs={{0,8},{1,9},{2,10},{3,11},{4,12},{5,13},{6,14},{7,15},{8,0},{9,1},... | collective-permute-start | bytes 196616 | tf_op jit(solution)/shard_map/ppermute | solution.py:60
  37.9 11.6 %collective-permute-start.8 = (bf16[32,2,512]{2,0,1:T(8,128)(2,1)S(1)}, bf16[32,2,512]{2,0,1:T(8,128)(2,1)S(1)}, u32[]{:S(2)}, u32[]{:S(2)}) collective-permute-start(bf16[32,2,512]{2,0,1:T(8,128)(2,1)S(1)} %get-tuple-element.14), channel_id=1, source_target_pairs={{0,9},{1,10},{2,11},{3,12},{4,13},{5,14},{6,15},{7,0},{8,1},{9,2},... | collective-permute-start | bytes 196616 | tf_op jit(solution)/shard_map/ppermute | solution.py:60
  44.8 8.1 %collective-permute-start.9 = (bf16[32,2,512]{2,0,1:T(8,128)(2,1)S(1)}, bf16[32,2,512]{2,0,1:T(8,128)(2,1)S(1)}, u32[]{:S(2)}, u32[]{:S(2)}) collective-permute-start(bf16[32,2,512]{2,0,1:T(8,128)(2,1)S(1)} %get-tuple-element.13), channel_id=1, source_target_pairs={{0,10},{1,11},{2,12},{3,13},{4,14},{5,15},{6,0},{7,1},{8,2},{9,3},... | collective-permute-start | bytes 196616 | tf_op jit(solution)/shard_map/ppermute | solution.py:60
  45.0 8.3 %collective-permute-start.10 = (bf16[32,2,512]{2,0,1:T(8,128)(2,1)S(1)}, bf16[32,2,512]{2,0,1:T(8,128)(2,1)S(1)}, u32[]{:S(2)}, u32[]{:S(2)}) collective-permute-start(bf16[32,2,512]{2,0,1:T(8,128)(2,1)S(1)} %get-tuple-element.12), channel_id=1, source_target_pairs={{0,11},{1,12},{2,13},{3,14},{4,15},{5,0},{6,1},{7,2},{8,3},{9,4},{... | collective-permute-start | bytes 196616 | tf_op jit(solution)/shard_map/ppermute | solution.py:60
  45.4 7.9 %collective-permute-start.11 = (bf16[32,2,512]{2,0,1:T(8,128)(2,1)S(1)}, bf16[32,2,512]{2,0,1:T(8,128)(2,1)S(1)}, u32[]{:S(2)}, u32[]{:S(2)}) collective-permute-start(bf16[32,2,512]{2,0,1:T(8,128)(2,1)S(1)} %get-tuple-element.11), channel_id=1, source_target_pairs={{0,12},{1,13},{2,14},{3,15},{4,0},{5,1},{6,2},{7,3},{8,4},{9,5},{1... | collective-permute-start | bytes 196616 | tf_op jit(solution)/shard_map/ppermute | solution.py:60
  47.3 6.1 %collective-permute-start.12 = (bf16[32,2,512]{2,0,1:T(8,128)(2,1)S(1)}, bf16[32,2,512]{2,0,1:T(8,128)(2,1)S(1)}, u32[]{:S(2)}, u32[]{:S(2)}) collective-permute-start(bf16[32,2,512]{2,0,1:T(8,128)(2,1)S(1)} %get-tuple-element.10), channel_id=1, source_target_pairs={{0,13},{1,14},{2,15},{3,0},{4,1},{5,2},{6,3},{7,4},{8,5},{9,6},{10... | collective-permute-start | bytes 196616 | tf_op jit(solution)/shard_map/ppermute | solution.py:60
  49.5 6.2 %collective-permute-start.13 = (bf16[32,2,512]{2,0,1:T(8,128)(2,1)S(1)}, bf16[32,2,512]{2,0,1:T(8,128)(2,1)S(1)}, u32[]{:S(2)}, u32[]{:S(2)}) collective-permute-start(bf16[32,2,512]{2,0,1:T(8,128)(2,1)S(1)} %get-tuple-element.9), channel_id=1, source_target_pairs={{0,14},{1,15},{2,0},{3,1},{4,2},{5,3},{6,4},{7,5},{8,6},{9,7},{10,... | collective-permute-start | bytes 196616 | tf_op jit(solution)/shard_map/ppermute | solution.py:60
  52.9 3.2 %collective-permute-start.14 = (bf16[32,2,512]{2,0,1:T(8,128)(2,1)S(1)}, bf16[32,2,512]{2,0,1:T(8,128)(2,1)S(1)}, u32[]{:S(2)}, u32[]{:S(2)}) collective-permute-start(bf16[32,2,512]{2,0,1:T(8,128)(2,1)S(1)} %get-tuple-element.8), channel_id=1, source_target_pairs={{0,15},{1,0},{2,1},{3,2},{4,3},{5,4},{6,5},{7,6},{8,7},{9,8},{10,9... | collective-permute-start | bytes 196616 | tf_op jit(solution)/shard_map/ppermute | solution.py:60
  56.2 142.9 %copy-start.1 = (s32[32]{0:T(128)S(1)}, s32[32]{0:T(128)}, u32[]{:S(2)}) copy-start(s32[32]{0:T(128)} %param.11) | copy-start | bytes 388
  57.8 180.4 %all-reduce.2.cloned.1.call-start = ((), (), s32[]{:S(2)}) async-start(), calls=%async_computation.2 | async-start | bytes 2097152 | tf_op jit(solution)/shard_map/psum | solution.py:45
Sparse Core Ops, SparseCore 0:
  18.9 180.0 reduce-scatter.1
Sparse Core Ops, SparseCore 1:
  57.9 34.2 all-gather.1
  199.1 39.0 all-reduce.1
